TPU v7x, 32 devices: a whole 2x2x4 slice. The times are simulated.
32 devices in a mesh: win: 8 (over z, x), fsdp: 4 (over y, core).
Axes of the slice: x: 2, y: 2, z: 4, core: 2. Of those that a mesh axis runs over, the one named last changes fastest.
Arguments:
- queries: bfloat16 [8192, 2560], P(('win', 'fsdp')), may hold values from -5 to 5
- keys: bfloat16 [8192, 2560], P(('win', 'fsdp')), may hold values from -5 to 5
- values: bfloat16 [8192, 2560], P(('win', 'fsdp')), may hold values from -6 to 6
- stream: bfloat16 [8192, 5120], P(('win', 'fsdp')), may hold values from -0.59765625 to 0.59765625
- out_weight: bfloat16 [2560, 5120], P('fsdp', 'win'), may hold values from -0.125 to 0.125
- gate: float32 [5120], replicated, may hold values from 0.5 to 2
- head_shift: float32 [5120], replicated, may hold values from -3 to 3
- head_scale: float32 [5120], replicated, may hold values from 0.25 to 1.75
- head_weight: bfloat16 [5120, 64], replicated, may hold values from -0.078125 to 0.078125
- latents: float32 [128, 4096], P('win', 'fsdp'), may hold values from -6 to 6
- step_size: float32 [1], replicated, may hold values from 0.5 to 1
- intersections: int32 [8], replicated, may hold values from 1 to 4
- ramps: int32 [8, 4, 2], replicated, may hold values from 1 to 16
Outputs:
- blended: float32 [128, 4096], P('win', 'fsdp')
All inputs are finite; a program needn't handle non-finite values.
Results may differ from a plain program's by a relative error of at most 0.0065.
Values may be sent and summed in bfloat16 or wider, within the bound.
A program may use at most 128 MiB of HBM per device.

v0:
```python
import math
import jax
import jax.numpy as jnp
from jax import lax
from jax.sharding import PartitionSpec as P

HEADS = 20
HD = 128
FD = 4
EPSILON = 0.001


def padded_2(value, sides, width):
    for axis, dim in sides:
        size, length = (lax.axis_size(axis), value.shape[dim])
        up = [(i, (i + 1) % size) for i in range(size)]
        down = [(j, i) for i, j in up]
        last = lax.slice_in_dim(value, length - width, length, axis=dim)
        initial = lax.slice_in_dim(value, 0, width, axis=dim)
        before = lax.ppermute(last, axis, up)
        after = lax.ppermute(initial, axis, down)
        value = jnp.concatenate([before, value, after], axis=dim)
    return value


def softmax_block(query_h, key_h, value_h, score_scale):
    scores = (
        jnp.einsum("qhd,khd->hqk", query_h, key_h, preferred_element_type=jnp.float32) * score_scale
    )
    highest = jnp.max(scores, axis=-1, keepdims=True)
    exponent = jnp.exp(scores - highest)
    denominator = jnp.sum(exponent, axis=-1)
    probability = exponent.astype(jnp.bfloat16)
    summed = jnp.einsum("hqk,khd->qhd", probability, value_h, preferred_element_type=jnp.float32)
    return summed / jnp.transpose(denominator)[:, :, None]


def local(
    queries,
    keys,
    values,
    stream,
    out_weight,
    gate,
    head_shift,
    head_scale,
    head_weight,
    latents,
    step_size,
    intersections,
    ramps,
):
    tok_rows, feat_width = queries.shape
    groups = lax.axis_size("fsdp")
    head_count = HEADS
    score_scale = 1.0 / math.sqrt(HD)
    per_group = head_count // groups
    split_shape = (tok_rows, groups, per_group, HD)
    query_part = lax.all_to_all(
        queries.reshape(split_shape), "fsdp", split_axis=1, concat_axis=0, tiled=True
    )
    key_part = lax.all_to_all(
        keys.reshape(split_shape), "fsdp", split_axis=1, concat_axis=0, tiled=True
    )
    value_part = lax.all_to_all(
        values.reshape(split_shape), "fsdp", split_axis=1, concat_axis=0, tiled=True
    )
    result = softmax_block(query_part[:, 0], key_part[:, 0], value_part[:, 0], score_scale)
    own_heads = result.astype(jnp.bfloat16)[:, None]
    window_rows = own_heads.shape[0]
    own_heads = own_heads.reshape(window_rows, per_group * HD)
    full_columns = lax.all_gather(out_weight, "win", axis=1, tiled=True)
    projected = lax.psum_scatter(
        jnp.dot(own_heads, full_columns, preferred_element_type=jnp.float32).astype(jnp.bfloat16),
        "fsdp",
        scatter_dimension=0,
        tiled=True,
    ).astype(jnp.float32)
    hidden = stream.astype(jnp.float32) + gate * projected
    centre = jnp.mean(hidden, axis=-1, keepdims=True)
    centred = hidden - centre
    variance = jnp.mean(centred * centred, axis=-1, keepdims=True)
    normed = centred / jnp.sqrt(variance + EPSILON)
    modulated = (normed * head_scale + head_shift).astype(jnp.bfloat16)
    velocity = jnp.dot(modulated, head_weight, preferred_element_type=jnp.float32)
    fresh = latents + step_size[0] * velocity.reshape(latents.shape)
    frames_dev = latents.shape[0]
    shared = FD
    padded = padded_2(fresh.astype(jnp.bfloat16), (("win", 0),), shared).astype(fresh.dtype)
    prev_block = padded[:shared]
    next_block = padded[shared + frames_dev :]
    window = lax.axis_index("win")
    win_count = lax.axis_size("win")
    prev_window = (window + win_count - 1) % win_count
    window_ids = jnp.arange(win_count, dtype=jnp.int32)
    over_prev = jnp.sum(jnp.where(window_ids == prev_window, intersections, 0))
    over_next = jnp.sum(jnp.where(window_ids == window, intersections, 0))
    ramp_prev = jnp.sum(
        jnp.where((window_ids == prev_window)[:, None, None], ramps, 0), axis=0
    ).astype(jnp.float32)
    ramp_own = jnp.sum(jnp.where((window_ids == window)[:, None, None], ramps, 0), axis=0).astype(
        jnp.float32
    )
    frame_ids = jnp.arange(frames_dev, dtype=jnp.int32)
    shared_ids = jnp.arange(shared, dtype=jnp.int32)
    inside_prev = frame_ids < over_prev
    select_prev = (
        (shared_ids[None, :] == shared - over_prev + frame_ids[:, None]) & inside_prev[:, None]
    ).astype(jnp.float32)
    prev_aligned = jnp.dot(select_prev, prev_block, precision=lax.Precision.HIGHEST)
    rows_prev = (shared_ids[None, :] == frame_ids[:, None]).astype(jnp.float32)
    ramp_rows_prev = jnp.dot(rows_prev, ramp_prev, precision=lax.Precision.HIGHEST)
    weight_before = ramp_rows_prev[:, 0:1]
    weight_self = ramp_rows_prev[:, 1:2]
    spare_prev = 1.0 - (frame_ids < shared).astype(jnp.float32)[:, None]
    blend_prev = (weight_before * prev_aligned + weight_self * fresh) / (
        weight_before + weight_self + spare_prev
    )
    shifted = frame_ids - (frames_dev - over_next)
    inside_next = shifted >= 0
    select_next = (shared_ids[None, :] == shifted[:, None]).astype(jnp.float32)
    next_aligned = jnp.dot(select_next, next_block, precision=lax.Precision.HIGHEST)
    ramp_rows = jnp.dot(select_next, ramp_own, precision=lax.Precision.HIGHEST)
    weight_mine = ramp_rows[:, 0:1]
    weight_after = ramp_rows[:, 1:2]
    spare = 1.0 - inside_next.astype(jnp.float32)[:, None]
    blend_next = (weight_mine * fresh + weight_after * next_aligned) / (
        weight_mine + weight_after + spare
    )
    return jnp.where(
        inside_prev[:, None], blend_prev, jnp.where(inside_next[:, None], blend_next, fresh)
    )


def solution(mesh):
    in_specs = (
        P(("win", "fsdp"), None),
        P(("win", "fsdp"), None),
        P(("win", "fsdp"), None),
        P(("win", "fsdp"), None),
        P("fsdp", "win"),
        P(),
        P(),
        P(),
        P(),
        P("win", "fsdp"),
        P(),
        P(),
        P(),
    )
    out_specs = P("win", "fsdp")
    return jax.shard_map(local, mesh=mesh, in_specs=in_specs, out_specs=out_specs, check_vma=False)
```

profile of v0, /device:TPU:0, one launch (start us, length us, event | category | flops | bytes accessed | tf_op | source)
XLA Modules:
  0.0 235.3 jit_solution(2147026987415011485)
XLA Ops:
  7.3 2.4 %copy.18 = bf16[256,2560]{0,1:T(8,128)(2,1)} copy(bf16[256,2560]{1,0:T(8,128)(2,1)} %param.13) | data formatting | bytes 2621440 | tf_op args[0]
  9.7 4.3 %all-to-all-start = ((bf16[256,4,5,128]{0,3,2,1:T(8,128)(2,1)}), bf16[256,4,5,128]{0,3,2,1:T(8,128)(2,1)S(1)}, u32[]{:S(2)}, u32[]{:S(2)}) async-start(bf16[256,4,5,128]{0,3,2,1:T(8,128)(2,1)} %bitcast.2), calls=%async_computation | async-start | bytes 2621440 | tf_op jit(solution)/shard_map/all_to_all | solution.py:59
  14.0 1.4 copy.20
  15.4 15.8 %all-to-all-done = bf16[256,4,5,128]{0,3,2,1:T(8,128)(2,1)S(1)} async-done(((bf16[256,4,5,128]{0,3,2,1:T(8,128)(2,1)}), bf16[256,4,5,128]{0,3,2,1:T(8,128)(2,1)S(1)}, u32[]{:S(2)}, u32[]{:S(2)}) %all-to-all-start) | async-done | bytes 1310752 | tf_op jit(solution)/shard_map/all_to_all | solution.py:59
  31.2 3.5 %all-to-all-start.1 = ((bf16[256,4,5,128]{0,3,2,1:T(8,128)(2,1)}), bf16[256,4,5,128]{0,3,2,1:T(8,128)(2,1)S(1)}, u32[]{:S(2)}, u32[]{:S(2)}) async-start(bf16[256,4,5,128]{0,3,2,1:T(8,128)(2,1)} %bitcast.49), calls=%async_computation.1 | async-start | bytes 2621440 | tf_op jit(solution)/shard_map/all_to_all | solution.py:62
  34.7 2.4 %copy.22 = bf16[256,2560]{0,1:T(8,128)(2,1)} copy(bf16[256,2560]{1,0:T(8,128)(2,1)} %param.15) | data formatting | bytes 2621440 | tf_op args[2]
  37.2 14.8 %all-to-all-done.1 = bf16[256,4,5,128]{0,3,2,1:T(8,128)(2,1)S(1)} async-done(((bf16[256,4,5,128]{0,3,2,1:T(8,128)(2,1)}), bf16[256,4,5,128]{0,3,2,1:T(8,128)(2,1)S(1)}, u32[]{:S(2)}, u32[]{:S(2)}) %all-to-all-start.1) | async-done | bytes 1310752 | tf_op jit(solution)/shard_map/all_to_all | solution.py:62
  52.0 4.3 %all-to-all-start.2 = ((bf16[256,4,5,128]{0,3,2,1:T(8,128)(2,1)}), bf16[256,4,5,128]{0,3,2,1:T(8,128)(2,1)}, u32[]{:S(2)}, u32[]{:S(2)}) async-start(bf16[256,4,5,128]{0,3,2,1:T(8,128)(2,1)} %bitcast.48), calls=%async_computation.2 | async-start | bytes 2621440 | tf_op jit(solution)/shard_map/all_to_all | solution.py:65
  57.1 1.8 copy.21
  58.9 14.7 %all-to-all-done.2 = bf16[256,4,5,128]{0,3,2,1:T(8,128)(2,1)} async-done(((bf16[256,4,5,128]{0,3,2,1:T(8,128)(2,1)}), bf16[256,4,5,128]{0,3,2,1:T(8,128)(2,1)}, u32[]{:S(2)}, u32[]{:S(2)}) %all-to-all-start.2) | async-done | bytes 1310752 | tf_op jit(solution)/shard_map/all_to_all | solution.py:65
  73.6 3.4 %copy.23 = bf16[4,256,1,5,128]{1,0,4,3,2:T(4,128)(2,1)} copy(bf16[4,256,1,5,128]{1,4,3,0,2:T(8,128)(2,1)} %bitcast.12) | data formatting | bytes 2621440 | tf_op jit(solution)/shard_map/all_to_all | solution.py:65
  77.0 3.7 %squeeze.15 = bf16[1024,5,128]{0,2,1:T(8,128)(2,1)} reshape(bf16[4,256,1,5,128]{1,0,4,3,2:T(4,128)(2,1)} %copy.23) | data formatting | bytes 2621440 | tf_op jit(solution)/shard_map/squeeze | solution.py:68
  80.6 2.9 %multiply_reduce_fusion = (f32[5,1024]{1,0:T(8,128)S(1)}, f32[5,1024,1024]{1,2,0:T(8,128)S(1)}) fusion(bf16[1024,5,128]{2,0,1:T(8,128)(2,1)S(1)} %bitcast.44, bf16[1024,5,128]{2,0,1:T(8,128)(2,1)S(1)} %bitcast.45), kind=kOutput, calls=%fused_computation.1 | convolution fusion | flops 1352657920 | bytes 23613440 | tf_op jit(solution)/shard_map/qhd,khd->hqk/dot_general | solution.py:28
  83.5 3.7 %fusion = f32[5,1024]{1,0:T(8,128)S(1)} fusion(f32[5,1024,1024]{1,2,0:T(8,128)S(1)} %get-tuple-element.20, f32[5,1024]{1,0:T(8,128)S(1)} %get-tuple-element.19), kind=kLoop, calls=%fused_computation.2 | loop fusion | flops 15723520 | bytes 21012480 | tf_op jit(solution)/shard_map/reduce_sum | solution.py:32
  87.2 3.7 %copy-done.1 = f32[5,1024,1024]{1,2,0:T(8,128)} copy-done((f32[5,1024,1024]{1,2,0:T(8,128)}, f32[5,1024,1024]{1,2,0:T(8,128)S(1)}, u32[]{:S(2)}) %copy-start.1) | copy-done | bytes 20971544
  91.0 11.2 %fusion.7 = bf16[1024,5,128]{0,2,1:T(8,128)(2,1)S(1)} fusion(bf16[1024,5,128]{0,2,1:T(8,128)(2,1)S(1)} %copy-done.6, f32[5,1024,1024]{1,2,0:T(8,128)} %copy-done.1, f32[5,1024]{1,0:T(8,128)S(1)} %get-tuple-element.19, f32[1024,5]{0,1:T(8,128)S(1)} %bitcast.50), kind=kOutput, calls=%fused_computation.13 | convolution fusion | flops 1359216640 | bytes 23633920 | tf_op jit(solution)/shard_map/hqk,khd->qhd/dot_general | solution.py:34
  102.2 12.1 %all-gather.2.cloned.1.call-done = bf16[640,5120]{1,0:T(8,128)(2,1)} async-done(((bf16[640,640]{1,0:T(8,128)(2,1)}), bf16[640,5120]{1,0:T(8,128)(2,1)}) %all-gather.2.cloned.1.call-update) | async-done | bytes 6553616 | tf_op jit(solution)/shard_map/all_gather | solution.py:72
  114.3 13.8 %convolution_convert_fusion = bf16[1024,5120]{1,0:T(8,128)(2,1)} fusion(bf16[1024,640]{0,1:T(8,128)(2,1)S(1)} %bitcast.51, bf16[640,5120]{1,0:T(8,128)(2,1)} %all-gather.2.cloned.1.call-done), kind=kOutput, calls=%fused_computation.7 | convolution fusion | flops 6716129280 | bytes 18350080 | tf_op jit(solution)/shard_map/dot_general | solution.py:74
  132.2 78.6 %reduce-scatter.2.cloned.1.call-done = bf16[256,5120]{1,0:T(8,128)(2,1)} async-done(((bf16[1024,5120]{1,0:T(8,128)(2,1)}), bf16[256,5120]{1,0:T(8,128)(2,1)}) %reduce-scatter.2.cloned.1.call-update) | async-done | bytes 2621456 | tf_op jit(solution)/shard_map/reduce_scatter | solution.py:73
  210.9 2.8 %fusion.6 = f32[256]{0:T(256)S(1)} fusion(bf16[256,5120]{1,0:T(8,128)(2,1)} %reduce-scatter.2.cloned.1.call-done, bf16[256,5120]{1,0:T(8,128)(2,1)S(1)} %copy-done.2, f32[5120]{0:T(1024)S(1)} %copy-done.7), kind=kLoop, calls=%fused_computation.11 | loop fusion | flops 6553344 | bytes 5264384 | tf_op jit(solution)/shard_map/reduce_sum | solution.py:80
  215.1 1.7 fusion.17
  217.0 4.3 %collective-permute-start.1 = (bf16[4,1024]{1,0:T(4,128)(2,1)S(1)}, bf16[4,1024]{1,0:T(4,128)(2,1)S(1)}, u32[]{:S(2)}, u32[]{:S(2)}) collective-permute-start(bf16[4,1024]{1,0:T(4,128)(2,1)S(1)} %get-tuple-element.12), channel_id=1, source_target_pairs={{4,0},{8,4},{12,8},{16,12},{20,16},{24,20},{28,24},{0,28},{5,1},{9... | collective-permute-start | bytes 24584 | tf_op jit(solution)/shard_map/ppermute | solution.py:21
  221.3 1.4 collective-permute-done.1
  222.9 4.8 %collective-permute-done = bf16[4,1024]{1,0:T(4,128)(2,1)S(1)} collective-permute-done((bf16[4,1024]{1,0:T(4,128)(2,1)S(1)}, bf16[4,1024]{1,0:T(4,128)(2,1)S(1)}, u32[]{:S(2)}, u32[]{:S(2)}) %collective-permute-start) | collective-permute-done | bytes 8224 | tf_op jit(solution)/shard_map/ppermute | solution.py:20
  (51 shorter events, 6.1 us)
Async XLA Ops:
  6.5 208.5 %copy-start = (bf16[5120,64]{0,1:T(8,128)(2,1)S(1)}, bf16[5120,64]{0,1:T(8,128)(2,1)}, u32[]{:S(2)}) copy-start(bf16[5120,64]{0,1:T(8,128)(2,1)} %param.21) | copy-start | bytes 1966084
  6.5 7.4 %copy-start.5 = (bf16[256,2560]{1,0:T(8,128)(2,1)S(1)}, bf16[256,2560]{1,0:T(8,128)(2,1)}, u32[]{:S(2)}) copy-start(bf16[256,2560]{1,0:T(8,128)(2,1)} %param.14) | copy-start | bytes 3932164
  6.5 107.7 %all-gather.2.cloned.1.call-start = ((), (), s32[]{:S(2)}) async-start(), calls=%async_computation.4 | async-start | bytes 7372800 | tf_op jit(solution)/shard_map/all_gather | solution.py:72
  9.7 21.5 %all-to-all-start = ((bf16[256,4,5,128]{0,3,2,1:T(8,128)(2,1)}), bf16[256,4,5,128]{0,3,2,1:T(8,128)(2,1)S(1)}, u32[]{:S(2)}, u32[]{:S(2)}) async-start(bf16[256,4,5,128]{0,3,2,1:T(8,128)(2,1)} %bitcast.2), calls=%async_computation | async-start | bytes 2621440 | tf_op jit(solution)/shard_map/all_to_all | solution.py:59
  31.2 20.8 %all-to-all-start.1 = ((bf16[256,4,5,128]{0,3,2,1:T(8,128)(2,1)}), bf16[256,4,5,128]{0,3,2,1:T(8,128)(2,1)S(1)}, u32[]{:S(2)}, u32[]{:S(2)}) async-start(bf16[256,4,5,128]{0,3,2,1:T(8,128)(2,1)} %bitcast.49), calls=%async_computation.1 | async-start | bytes 2621440 | tf_op jit(solution)/shard_map/all_to_all | solution.py:62
  52.0 4.4 %copy-start.4 = (bf16[256,4,5,128]{0,3,2,1:T(8,128)(2,1)}, bf16[256,4,5,128]{0,3,2,1:T(8,128)(2,1)S(1)}, u32[]{:S(2)}) copy-start(bf16[256,4,5,128]{0,3,2,1:T(8,128)(2,1)S(1)} %all-to-all-done.1) | copy-start | bytes 3932164
  52.0 21.6 %all-to-all-start.2 = ((bf16[256,4,5,128]{0,3,2,1:T(8,128)(2,1)}), bf16[256,4,5,128]{0,3,2,1:T(8,128)(2,1)}, u32[]{:S(2)}, u32[]{:S(2)}) async-start(bf16[256,4,5,128]{0,3,2,1:T(8,128)(2,1)} %bitcast.48), calls=%async_computation.2 | async-start | bytes 2621440 | tf_op jit(solution)/shard_map/all_to_all | solution.py:65
  56.3 154.6 %reduce-scatter.2.cloned.1.call-start = ((), (), s32[]{:S(2)}) async-start(), calls=%async_computation.5 | async-start | bytes 13107200 | tf_op jit(solution)/shard_map/reduce_scatter | solution.py:73
  83.5 7.4 %copy-start.1 = (f32[5,1024,1024]{1,2,0:T(8,128)}, f32[5,1024,1024]{1,2,0:T(8,128)S(1)}, u32[]{:S(2)}) copy-start(f32[5,1024,1024]{1,2,0:T(8,128)S(1)} %get-tuple-element.20) | copy-start | bytes 62914564
  83.5 7.4 %copy-start.6 = (bf16[1024,5,128]{0,2,1:T(8,128)(2,1)S(1)}, bf16[1024,5,128]{0,2,1:T(8,128)(2,1)}, u32[]{:S(2)}) copy-start(bf16[1024,5,128]{0,2,1:T(8,128)(2,1)} %squeeze.15) | copy-start | bytes 3932164
  128.1 0.9 copy-start.10
  128.1 3.5 %copy-start.9 = (s32[8,4,2]{0,2,1:T(2,128)S(1)}, s32[8,4,2]{0,2,1:T(2,128)}, u32[]{:S(2)}) copy-start(s32[8,4,2]{0,2,1:T(2,128)} %param.25) | copy-start | bytes 772
  128.1 82.8 %copy-start.2 = (bf16[256,5120]{1,0:T(8,128)(2,1)S(1)}, bf16[256,5120]{1,0:T(8,128)(2,1)}, u32[]{:S(2)}) copy-start(bf16[256,5120]{1,0:T(8,128)(2,1)} %param.16) | copy-start | bytes 7864324
  128.1 82.8 %copy-start.7 = (f32[5120]{0:T(1024)S(1)}, f32[5120]{0:T(1024)}, u32[]{:S(2)}) copy-start(f32[5120]{0:T(1024)} %param.18) | copy-start | bytes 61444
  132.2 82.8 %copy-start.11 = (f32[5120]{0:T(1024)S(1)}, f32[5120]{0:T(1024)}, u32[]{:S(2)}) copy-start(f32[5120]{0:T(1024)} %param.19) | copy-start | bytes 61444
  132.2 82.8 %copy-start.12 = (f32[5120]{0:T(1024)S(1)}, f32[5120]{0:T(1024)}, u32[]{:S(2)}) copy-start(f32[5120]{0:T(1024)} %param.20) | copy-start | bytes 61444
  210.9 2.8 %copy-start.3 = (bf16[256,5120]{1,0:T(8,128)(2,1)S(1)}, bf16[256,5120]{1,0:T(8,128)(2,1)}, u32[]{:S(2)}) copy-start(bf16[256,5120]{1,0:T(8,128)(2,1)} %reduce-scatter.2.cloned.1.call-done) | copy-start | bytes 7864324
  215.0 1.9 copy-start.8
  217.0 5.7 %collective-permute-start.1 = (bf16[4,1024]{1,0:T(4,128)(2,1)S(1)}, bf16[4,1024]{1,0:T(4,128)(2,1)S(1)}, u32[]{:S(2)}, u32[]{:S(2)}) collective-permute-start(bf16[4,1024]{1,0:T(4,128)(2,1)S(1)} %get-tuple-element.12), channel_id=1, source_target_pairs={{4,0},{8,4},{12,8},{16,12},{20,16},{24,20},{28,24},{0,28},{5,1},{9... | collective-permute-start | bytes 24584 | tf_op jit(solution)/shard_map/ppermute | solution.py:21
  221.3 6.3 %collective-permute-start = (bf16[4,1024]{1,0:T(4,128)(2,1)S(1)}, bf16[4,1024]{1,0:T(4,128)(2,1)S(1)}, u32[]{:S(2)}, u32[]{:S(2)}) collective-permute-start(bf16[4,1024]{1,0:T(4,128)(2,1)S(1)} %get-tuple-element.11), channel_id=1, source_target_pairs={{0,4},{4,8},{8,12},{12,16},{16,20},{20,24},{24,28},{28,0},{1,5},{5... | collective-permute-start | bytes 24584 | tf_op jit(solution)/shard_map/ppermute | solution.py:20
Sparse Core Ops, SparseCore 0:
  9.6 104.6 all-gather.1
  128.3 82.5 reduce-scatter.1
where the time goes:
time: 236 us; the launch traced here: 235 us
  waiting for transfers between devices  143 us (61%)
  matrix products  31 us (13%)
  local copies, waits for them, and re-layouts  19.9 us (8%)
  starting transfers between devices  16.5 us (7%)
  between operations  15.7 us (7%)
  other arithmetic  9.4 us (4%)
    reduce_scatter x1, waiting for transfers between devices, local(): lax.psum_scatter(jnp.dot(own_heads, full_columns, preferred_element_type=...  78.6 us
    all_to_all x1, waiting for transfers between devices, local(): lax.all_to_all(queries.reshape(split_shape), 'fsdp', split_axis=1, concat...  15.8 us
    all_to_all x1, waiting for transfers between devices, local(): lax.all_to_all(keys.reshape(split_shape), 'fsdp', split_axis=1, concat_ax...  14.8 us
    all_to_all x1, waiting for transfers between devices, local(): lax.all_to_all(values.reshape(split_shape), 'fsdp', split_axis=1, concat_...  14.7 us
    dot_general x1, matrix products, local(): jnp.dot(own_heads, full_columns, preferred_element_type=jnp.float32)  13.8 us
    all_gather x1, waiting for transfers between devices, local(): full_columns = lax.all_gather(out_weight, 'win', axis=1, tiled=True)  12.1 us
    dot_general x1, matrix products, softmax_block(): jnp.einsum('hqk,khd->qhd', probability, value_h, preferred_element_type=j...  11.2 us
    unnamed x29, local copies, waits for them, and re-layouts  10.1 us
  transfers between devices with their start and end apart: 7, of which 7 were waited for; matrix products, arithmetic and copies ran while one was open for 15% of the time, Pallas kernels for 0%

commit v1 on v0

--- a/solution.py
+++ b/solution.py
@@ -8,6 +8,24 @@
 HD = 128
 FD = 4
 EPSILON = 0.001
+
+
+def in_order(pieces, dim):
+    pieces = jnp.moveaxis(pieces, 0, dim)
+    shape = pieces.shape
+    return pieces.reshape(*shape[:dim], shape[dim] * shape[dim + 1], *shape[dim + 2 :])
+
+
+def collected_by_bits(value, axis):
+    size = lax.axis_size(axis)
+    blocks = value[None]
+    for level in range(size.bit_length() - 1):
+        bit = 1 << level
+        other = lax.ppermute(blocks, axis, [(i, i ^ bit) for i in range(size)])
+        both = jnp.stack([blocks, other])
+        upper = lax.axis_index(axis) >> level & 1
+        blocks = jnp.where(upper == 0, both, both[::-1]).reshape(-1, *value.shape)
+    return blocks
 
 
 def padded_2(value, sides, width):
@@ -69,7 +87,7 @@
     own_heads = result.astype(jnp.bfloat16)[:, None]
     window_rows = own_heads.shape[0]
     own_heads = own_heads.reshape(window_rows, per_group * HD)
-    full_columns = lax.all_gather(out_weight, "win", axis=1, tiled=True)
+    full_columns = in_order(collected_by_bits(out_weight, "win"), 1)
     projected = lax.psum_scatter(
         jnp.dot(own_heads, full_columns, preferred_element_type=jnp.float32).astype(jnp.bfloat16),
         "fsdp",

time: 236 us -> 358 us (1.52)
  waiting for transfers between devices: 143 us -> 233 us
  local copies, waits for them, and re-layouts: 19.9 us -> 34 us
  other arithmetic: 9.4 us -> 21.6 us
  starting transfers between devices: 16.5 us -> 24.5 us
    ppermute x0 -> x3, waiting for transfers between devices: none -> 115 us  [collected_by_bits(): other = lax.ppermute(blocks, axis, [(i, i ^ bit) for i in range(size)])]
    all_gather x1 -> x0, waiting for transfers between devices: 12.1 us -> none  [local(): full_columns = lax.all_gather(out_weight, 'win', axis=1, tiled=True)]
    another operation x0 -> x4, other arithmetic: none -> 8.49 us  [collected_by_bits(): both = jnp.stack([blocks, other])]
    ppermute x0 -> x3, starting transfers between devices: none -> 7.37 us  [collected_by_bits(): other = lax.ppermute(blocks, axis, [(i, i ^ bit) for i in range(size)])]
    all_to_all x1, waiting for transfers between devices: 14.8 us -> 7.64 us  [local(): lax.all_to_all(keys.reshape(split_shape), 'fsdp', split_axis=1, concat_ax...]
    all_to_all x1, waiting for transfers between devices: 15.8 us -> 9.38 us  [local(): lax.all_to_all(queries.reshape(split_shape), 'fsdp', split_axis=1, concat...]
    reshape x0 -> x1, local copies, waits for them, and re-layouts: none -> 5.86 us  [collected_by_bits(): blocks = jnp.where(upper == 0, both, both[::-1]).reshape(-1, *value.shape)]
    another operation x0 -> x1, local copies, waits for them, and re-layouts: none -> 5.68 us  [collected_by_bits(): both = jnp.stack([blocks, other])]
  transfers between devices with their start and end apart: 7 -> 9, of which waited for: 7 -> 8; matrix products, arithmetic and copies ran while one was open for 15% -> 12% of each run, Pallas kernels for 0% -> 0%
where the time goes in v1:
time: 358 us; the launch traced here: 357 us
  waiting for transfers between devices  233 us (65%)
  local copies, waits for them, and re-layouts  34 us (9%)
  matrix products  28 us (8%)
  starting transfers between devices  24.5 us (7%)
  other arithmetic  21.6 us (6%)
  between operations  15.7 us (4%)
    ppermute x3, waiting for transfers between devices, collected_by_bits(): other = lax.ppermute(blocks, axis, [(i, i ^ bit) for i in range(size)])  115 us
    reduce_scatter x1, waiting for transfers between devices, local(): lax.psum_scatter(jnp.dot(own_heads, full_columns, preferred_element_type=...  81.4 us
    all_to_all x1, waiting for transfers between devices, local(): lax.all_to_all(values.reshape(split_shape), 'fsdp', split_axis=1, concat_...  13.5 us
    dot_general x1, matrix products, local(): jnp.dot(own_heads, full_columns, preferred_element_type=jnp.float32)  11.1 us
    dot_general x1, matrix products, softmax_block(): jnp.einsum('hqk,khd->qhd', probability, value_h, preferred_element_type=j...  10.9 us
    unnamed x33, local copies, waits for them, and re-layouts  10.2 us
    all_to_all x1, waiting for transfers between devices, local(): lax.all_to_all(queries.reshape(split_shape), 'fsdp', split_axis=1, concat...  9.38 us
    another operation x4, other arithmetic, collected_by_bits(): both = jnp.stack([blocks, other])  8.49 us
  transfers between devices with their start and end apart: 9, of which 8 were waited for; matrix products, arithmetic and copies ran while one was open for 12% of the time, Pallas kernels for 0%

profile of v1, /device:TPU:0, one launch (start us, length us, event | category | flops | bytes accessed | tf_op | source)
XLA Modules:
  0.0 357.1 jit_solution(2007542536591520311)
XLA Ops:
  6.5 2.6 copy.22
  9.1 4.3 %all-to-all-start.2 = ((bf16[256,4,5,128]{0,3,2,1:T(8,128)(2,1)}), bf16[256,4,5,128]{0,3,2,1:T(8,128)(2,1)S(1)}, u32[]{:S(2)}, u32[]{:S(2)}) async-start(bf16[256,4,5,128]{0,3,2,1:T(8,128)(2,1)} %bitcast.10), calls=%async_computation.2 | async-start | bytes 2621440 | tf_op jit(solution)/shard_map/all_to_all | solution.py:83
  17.1 13.5 %all-to-all-done.2 = bf16[256,4,5,128]{0,3,2,1:T(8,128)(2,1)S(1)} async-done(((bf16[256,4,5,128]{0,3,2,1:T(8,128)(2,1)}), bf16[256,4,5,128]{0,3,2,1:T(8,128)(2,1)S(1)}, u32[]{:S(2)}, u32[]{:S(2)}) %all-to-all-start.2) | async-done | bytes 1310752 | tf_op jit(solution)/shard_map/all_to_all | solution.py:83
  30.6 4.3 %all-to-all-start = ((bf16[256,4,5,128]{0,3,2,1:T(8,128)(2,1)}), bf16[256,4,5,128]{0,3,2,1:T(8,128)(2,1)}, u32[]{:S(2)}, u32[]{:S(2)}) async-start(bf16[256,4,5,128]{0,3,2,1:T(8,128)(2,1)} %bitcast.2), calls=%async_computation | async-start | bytes 2621440 | tf_op jit(solution)/shard_map/all_to_all | solution.py:77
  40.4 2.5 copy.20
  42.8 9.4 %all-to-all-done = bf16[256,4,5,128]{0,3,2,1:T(8,128)(2,1)} async-done(((bf16[256,4,5,128]{0,3,2,1:T(8,128)(2,1)}), bf16[256,4,5,128]{0,3,2,1:T(8,128)(2,1)}, u32[]{:S(2)}, u32[]{:S(2)}) %all-to-all-start) | async-done | bytes 1310752 | tf_op jit(solution)/shard_map/all_to_all | solution.py:77
  52.2 4.3 %all-to-all-start.1 = ((bf16[256,4,5,128]{0,3,2,1:T(8,128)(2,1)}), bf16[256,4,5,128]{0,3,2,1:T(8,128)(2,1)}, u32[]{:S(2)}, u32[]{:S(2)}) async-start(bf16[256,4,5,128]{0,3,2,1:T(8,128)(2,1)} %bitcast.66), calls=%async_computation.1 | async-start | bytes 2621440 | tf_op jit(solution)/shard_map/all_to_all | solution.py:80
  56.6 3.5 copy.23
  60.1 3.7 %squeeze.15 = bf16[1024,5,128]{0,2,1:T(8,128)(2,1)} reshape(bf16[4,256,1,5,128]{1,0,4,3,2:T(4,128)(2,1)} %copy.23) | data formatting | bytes 2621440 | tf_op jit(solution)/shard_map/squeeze | solution.py:86
  66.2 7.6 %all-to-all-done.1 = bf16[256,4,5,128]{0,3,2,1:T(8,128)(2,1)} async-done(((bf16[256,4,5,128]{0,3,2,1:T(8,128)(2,1)}), bf16[256,4,5,128]{0,3,2,1:T(8,128)(2,1)}, u32[]{:S(2)}, u32[]{:S(2)}) %all-to-all-start.1) | async-done | bytes 1310752 | tf_op jit(solution)/shard_map/all_to_all | solution.py:80
  81.2 5.9 %copy.25 = bf16[4,640,640]{1,2,0:T(8,128)(2,1)} copy(bf16[4,640,640]{2,1,0:T(8,128)(2,1)} %bitcast.60) | data formatting | bytes 6553600 | tf_op jit(solution)/shard_map/reshape | solution.py:27
  87.1 2.8 collective-permute-start.2
  89.9 2.9 multiply_reduce_fusion
  92.8 3.7 %fusion = f32[5,1024]{1,0:T(8,128)S(1)} fusion(f32[5,1024,1024]{1,2,0:T(8,128)S(1)} %get-tuple-element.22, f32[5,1024]{1,0:T(8,128)S(1)} %get-tuple-element.21), kind=kLoop, calls=%fused_computation.2 | loop fusion | flops 15723520 | bytes 21012480 | tf_op jit(solution)/shard_map/reduce_sum | solution.py:50
  96.5 3.7 %copy-done.1 = f32[5,1024,1024]{1,2,0:T(8,128)} copy-done((f32[5,1024,1024]{1,2,0:T(8,128)}, f32[5,1024,1024]{1,2,0:T(8,128)S(1)}, u32[]{:S(2)}) %copy-start.1) | copy-done | bytes 20971544
  100.1 10.9 %fusion.7 = bf16[1024,5,128]{0,2,1:T(8,128)(2,1)S(1)} fusion(bf16[1024,5,128]{0,2,1:T(8,128)(2,1)S(1)} %copy-done.8, f32[5,1024,1024]{1,2,0:T(8,128)} %copy-done.1, f32[5,1024]{1,0:T(8,128)S(1)} %get-tuple-element.21, f32[1024,5]{0,1:T(8,128)S(1)} %bitcast.69), kind=kOutput, calls=%fused_computation.17 | convolution fusion | flops 1359216640 | bytes 23633920 | tf_op jit(solution)/shard_map/hqk,khd->qhd/dot_general | solution.py:52
  111.1 5.7 %copy.26 = bf16[1,4,640,640]{2,3,1,0:T(8,128)(2,1)} copy(bf16[1,4,640,640]{3,2,1,0:T(8,128)(2,1)} %bitcast.61) | data formatting | bytes 6553600 | tf_op jit(solution)/shard_map/stack;reshape | solution.py:25
  116.8 114.4 %collective-permute-done.2 = bf16[4,640,640]{1,2,0:T(8,128)(2,1)} collective-permute-done((bf16[4,640,640]{1,2,0:T(8,128)(2,1)}, bf16[4,640,640]{1,2,0:T(8,128)(2,1)}, u32[]{:S(2)}, u32[]{:S(2)}) %collective-permute-start.2) | collective-permute-done | bytes 3276832 | tf_op jit(solution)/shard_map/ppermute | solution.py:24
  231.2 3.6 %pad_maximum_fusion = bf16[2,4,640,640]{2,3,1,0:T(8,128)(2,1)S(1)} fusion(bf16[1,4,640,640]{2,3,1,0:T(8,128)(2,1)} %bitcast.24, bf16[1,4,640,640]{2,3,1,0:T(8,128)(2,1)} %copy.26), kind=kLoop, calls=%fused_computation.9 | loop fusion | flops 3276800 | bytes 13107200 | tf_op jit(solution)/shard_map/stack | solution.py:25
  236.1 11.1 %convolution_convert_fusion = bf16[1024,5120]{1,0:T(8,128)(2,1)} fusion(bf16[1024,640]{0,1:T(8,128)(2,1)S(1)} %bitcast.70, bf16[640,5120]{0,1:T(8,128)(2,1)S(1)} %bitcast.62), kind=kOutput, calls=%fused_computation.8 | convolution fusion | flops 6716129280 | bytes 18350080 | tf_op jit(solution)/shard_map/dot_general | solution.py:92
  251.3 81.4 %reduce-scatter.2.cloned.1.call-done = bf16[256,5120]{1,0:T(8,128)(2,1)} async-done(((bf16[1024,5120]{1,0:T(8,128)(2,1)}), bf16[256,5120]{1,0:T(8,128)(2,1)}) %reduce-scatter.2.cloned.1.call-update) | async-done | bytes 2621456 | tf_op jit(solution)/shard_map/reduce_scatter | solution.py:91
  332.6 2.8 fusion.6
  338.8 4.3 %collective-permute-start.4 = (bf16[4,1024]{1,0:T(4,128)(2,1)S(1)}, bf16[4,1024]{1,0:T(4,128)(2,1)S(1)}, u32[]{:S(2)}, u32[]{:S(2)}) collective-permute-start(bf16[4,1024]{1,0:T(4,128)(2,1)S(1)} %get-tuple-element.14), channel_id=1, source_target_pairs={{4,0},{8,4},{12,8},{16,12},{20,16},{24,20},{28,24},{0,28},{5,1},{9... | collective-permute-start | bytes 24584 | tf_op jit(solution)/shard_map/ppermute | solution.py:39
  344.6 4.8 %collective-permute-done.3 = bf16[4,1024]{1,0:T(4,128)(2,1)S(1)} collective-permute-done((bf16[4,1024]{1,0:T(4,128)(2,1)S(1)}, bf16[4,1024]{1,0:T(4,128)(2,1)S(1)}, u32[]{:S(2)}, u32[]{:S(2)}) %collective-permute-start.3) | collective-permute-done | bytes 8224 | tf_op jit(solution)/shard_map/ppermute | solution.py:38
  (66 shorter events, 28.0 us)
Async XLA Ops:
  6.5 330.3 %copy-start = (bf16[5120,64]{0,1:T(8,128)(2,1)S(1)}, bf16[5120,64]{0,1:T(8,128)(2,1)}, u32[]{:S(2)}) copy-start(bf16[5120,64]{0,1:T(8,128)(2,1)} %param.21) | copy-start | bytes 1966084
  6.5 9.2 %copy-start.7 = (bf16[256,2560]{1,0:T(8,128)(2,1)S(1)}, bf16[256,2560]{1,0:T(8,128)(2,1)}, u32[]{:S(2)}) copy-start(bf16[256,2560]{1,0:T(8,128)(2,1)} %param.13) | copy-start | bytes 3932164
  9.1 21.5 %all-to-all-start.2 = ((bf16[256,4,5,128]{0,3,2,1:T(8,128)(2,1)}), bf16[256,4,5,128]{0,3,2,1:T(8,128)(2,1)S(1)}, u32[]{:S(2)}, u32[]{:S(2)}) async-start(bf16[256,4,5,128]{0,3,2,1:T(8,128)(2,1)} %bitcast.10), calls=%async_computation.2 | async-start | bytes 2621440 | tf_op jit(solution)/shard_map/all_to_all | solution.py:83
  13.4 21.5 %collective-permute-start = (bf16[1,640,640]{2,1,0:T(8,128)(2,1)}, bf16[1,640,640]{2,1,0:T(8,128)(2,1)}, u32[]{:S(2)}, u32[]{:S(2)}) collective-permute-start(bf16[1,640,640]{2,1,0:T(8,128)(2,1)} %bitcast.67), channel_id=1, source_target_pairs={{0,4},{4,0},{8,12},{12,8},{16,20},{20,16},{24,28},{28,24},{1,5},{5... | collective-permute-start | bytes 2457608 | tf_op jit(solution)/shard_map/ppermute | solution.py:24
  30.6 4.3 %copy-start.6 = (bf16[256,4,5,128]{0,3,2,1:T(8,128)(2,1)}, bf16[256,4,5,128]{0,3,2,1:T(8,128)(2,1)S(1)}, u32[]{:S(2)}) copy-start(bf16[256,4,5,128]{0,3,2,1:T(8,128)(2,1)S(1)} %all-to-all-done.2) | copy-start | bytes 3932164
  30.6 21.6 %all-to-all-start = ((bf16[256,4,5,128]{0,3,2,1:T(8,128)(2,1)}), bf16[256,4,5,128]{0,3,2,1:T(8,128)(2,1)}, u32[]{:S(2)}, u32[]{:S(2)}) async-start(bf16[256,4,5,128]{0,3,2,1:T(8,128)(2,1)} %bitcast.2), calls=%async_computation | async-start | bytes 2621440 | tf_op jit(solution)/shard_map/all_to_all | solution.py:77
  38.1 39.0 %collective-permute-start.1 = (bf16[2,640,640]{2,1,0:T(8,128)(2,1)}, bf16[2,640,640]{2,1,0:T(8,128)(2,1)}, u32[]{:S(2)}, u32[]{:S(2)}) collective-permute-start(bf16[2,640,640]{2,1,0:T(8,128)(2,1)} %get-tuple-element.12), channel_id=1, source_target_pairs={{0,8},{4,12},{8,0},{12,4},{16,24},{20,28},{24,16},{28,20},{1,9},{5... | collective-permute-start | bytes 4915208 | tf_op jit(solution)/shard_map/ppermute | solution.py:24
  52.2 21.6 %all-to-all-start.1 = ((bf16[256,4,5,128]{0,3,2,1:T(8,128)(2,1)}), bf16[256,4,5,128]{0,3,2,1:T(8,128)(2,1)}, u32[]{:S(2)}, u32[]{:S(2)}) async-start(bf16[256,4,5,128]{0,3,2,1:T(8,128)(2,1)} %bitcast.66), calls=%async_computation.1 | async-start | bytes 2621440 | tf_op jit(solution)/shard_map/all_to_all | solution.py:80
  56.5 276.1 %reduce-scatter.2.cloned.1.call-start = ((), (), s32[]{:S(2)}) async-start(), calls=%async_computation.4 | async-start | bytes 13107200 | tf_op jit(solution)/shard_map/reduce_scatter | solution.py:91
  81.2 8.6 %copy-start.4 = (bf16[4,256,1,5,128]{4,1,0,3,2:T(8,128)(2,1)S(1)}, bf16[4,256,1,5,128]{4,1,0,3,2:T(8,128)(2,1)}, u32[]{:S(2)}) copy-start(bf16[4,256,1,5,128]{4,1,0,3,2:T(8,128)(2,1)} %copy.19) | copy-start | bytes 3932164
  81.2 8.6 %copy-start.5 = (bf16[4,256,1,5,128]{4,1,0,3,2:T(8,128)(2,1)S(1)}, bf16[4,256,1,5,128]{4,1,0,3,2:T(8,128)(2,1)}, u32[]{:S(2)}) copy-start(bf16[4,256,1,5,128]{4,1,0,3,2:T(8,128)(2,1)} %copy.21) | copy-start | bytes 3932164
  87.1 144.1 %collective-permute-start.2 = (bf16[4,640,640]{1,2,0:T(8,128)(2,1)}, bf16[4,640,640]{1,2,0:T(8,128)(2,1)}, u32[]{:S(2)}, u32[]{:S(2)}) collective-permute-start(bf16[4,640,640]{1,2,0:T(8,128)(2,1)} %copy.25), channel_id=1, source_target_pairs={{0,16},{4,20},{8,24},{12,28},{16,0},{20,4},{24,8},{28,12},{1,17},{... | collective-permute-start | bytes 9830408 | tf_op jit(solution)/shard_map/ppermute | solution.py:24
  92.8 7.4 %copy-start.1 = (f32[5,1024,1024]{1,2,0:T(8,128)}, f32[5,1024,1024]{1,2,0:T(8,128)S(1)}, u32[]{:S(2)}) copy-start(f32[5,1024,1024]{1,2,0:T(8,128)S(1)} %get-tuple-element.22) | copy-start | bytes 62914564
  92.8 7.4 %copy-start.8 = (bf16[1024,5,128]{0,2,1:T(8,128)(2,1)S(1)}, bf16[1024,5,128]{0,2,1:T(8,128)(2,1)}, u32[]{:S(2)}) copy-start(bf16[1024,5,128]{0,2,1:T(8,128)(2,1)} %squeeze.15) | copy-start | bytes 3932164
  247.2 0.8 copy-start.12
  247.2 3.4 copy-start.11
  247.2 85.4 %copy-start.2 = (bf16[256,5120]{1,0:T(8,128)(2,1)S(1)}, bf16[256,5120]{1,0:T(8,128)(2,1)}, u32[]{:S(2)}) copy-start(bf16[256,5120]{1,0:T(8,128)(2,1)} %param.16) | copy-start | bytes 7864324
  247.2 85.4 %copy-start.9 = (f32[5120]{0:T(1024)S(1)}, f32[5120]{0:T(1024)}, u32[]{:S(2)}) copy-start(f32[5120]{0:T(1024)} %param.18) | copy-start | bytes 61444
  332.6 2.9 copy-start.3
  335.5 1.3 copy-start.13
  335.5 1.3 copy-start.14
  336.8 1.9 copy-start.10
  338.8 5.6 %collective-permute-start.4 = (bf16[4,1024]{1,0:T(4,128)(2,1)S(1)}, bf16[4,1024]{1,0:T(4,128)(2,1)S(1)}, u32[]{:S(2)}, u32[]{:S(2)}) collective-permute-start(bf16[4,1024]{1,0:T(4,128)(2,1)S(1)} %get-tuple-element.14), channel_id=1, source_target_pairs={{4,0},{8,4},{12,8},{16,12},{20,16},{24,20},{28,24},{0,28},{5,1},{9... | collective-permute-start | bytes 24584 | tf_op jit(solution)/shard_map/ppermute | solution.py:39
  343.0 6.3 %collective-permute-start.3 = (bf16[4,1024]{1,0:T(4,128)(2,1)S(1)}, bf16[4,1024]{1,0:T(4,128)(2,1)S(1)}, u32[]{:S(2)}, u32[]{:S(2)}) collective-permute-start(bf16[4,1024]{1,0:T(4,128)(2,1)S(1)} %get-tuple-element.13), channel_id=1, source_target_pairs={{0,4},{4,8},{8,12},{12,16},{16,20},{20,24},{24,28},{28,0},{1,5},{5... | collective-permute-start | bytes 24584 | tf_op jit(solution)/shard_map/ppermute | solution.py:38
Sparse Core Ops, SparseCore 0:
  247.4 85.2 reduce-scatter.1
